TPU v7x, 32 devices: a whole 2x2x4 slice. The times are simulated.
32 devices in a mesh: sub: 8 (over z, x), grp: 4 (over y, core).
Axes of the slice: x: 2, y: 2, z: 4, core: 2. Of those that a mesh axis runs over, the one named last changes fastest.
Arguments:
- solution: float32 [32, 128, 2048], P(('sub', 'grp')), may hold values from -6 to 6
- residual: float32 [32, 128, 2048], P(('sub', 'grp'))
- direction: float32 [32, 128, 2048], P(('sub', 'grp'))
- residual_product: float32 [128], replicated, may hold values from 65536 to 1310720
- neighbor_slots: int32 [32, 4], P(('sub', 'grp')), may hold values from 0 to 3, each once within a row
- coupling: bfloat16 [32, 96, 256, 128], P(('sub', 'grp')), may hold values from -0.375 to 0.375
- dirichlet_factor: bfloat16 [32, 96, 128, 128], P(('sub', 'grp')), may hold values from -0.5 to 0.5
- face_block: bfloat16 [32, 32, 128, 128], P(('sub', 'grp')), as said below
- neumann_factor: bfloat16 [32, 32, 128, 128], P(('sub', 'grp')), may hold values from -0.5 to 0.5
- primal_block: int32 [32, 128], P(('sub', 'grp')), may hold values from 0 to 31
- primal_basis: bfloat16 [32, 128, 128], P(('sub', 'grp')), may hold values from -1.5 to 1.5
- coarse_matrix: float32 [32, 9, 128, 128], P(('sub', 'grp')), may hold values from -0.17677669 to 0.17677669
- coarse_block_inverse: float32 [32, 128, 128], P(('sub', 'grp')), may hold values from -0.5 to 0.5
- coarse_pattern: int32 [32, 9], P(('sub', 'grp')), may hold values from 0 to 31, as said below
Outputs:
- new_solution: float32 [32, 128, 2048], P(('sub', 'grp'))
- new_residual: float32 [32, 128, 2048], P(('sub', 'grp'))
- new_direction: float32 [32, 128, 2048], P(('sub', 'grp'))
- new_product: float32 [128], replicated
Inputs may be any that keep to these rules, and one draw needn't show every extreme that they name: `neighbor_slots`: each row orders the four local face slots: entry d is the slot of the face toward direction d (sub lower, sub upper, grp lower, grp upper). `coarse_pattern`: row t names 9 different subdomains, the first of them t itself; subdomain s lies on the device of index s along sub+grp, and every entry lies within 2 positions of row t along sub, cyclically. `face_block`: each block is symmetric with every eigenvalue at least 0.5.
All inputs are finite; a program needn't handle non-finite values.
Results may differ from a plain program's by a relative error of at most 0.0003.
Values sent between devices are 32-bit elements; how exact they have to be, the bound alone decides.
A program may use at most 128 MiB of HBM per device.

v0:
```python
import jax
import jax.numpy as jnp
from jax import lax
from jax.sharding import PartitionSpec as P

REACH_SUBS = 2
highest_precision = lax.Precision.HIGHEST


def shifted(value, axis, steps):
    count = lax.axis_size(axis)
    pairs = [(source, (source + steps) % count) for source in range(count)]
    return lax.ppermute(value, axis, pairs)


def slot_table(neighbor_slots):
    return (neighbor_slots[0][:, None] == jnp.arange(4, dtype=jnp.int32)[None, :]).astype(
        jnp.float32
    )


def place_faces(directed, slot_onehot, block_width):
    load_count = directed.shape[1]
    face_width = directed.shape[2]
    placed = jnp.einsum("dk,dlf->lkf", slot_onehot, directed, precision=highest_precision)
    return placed.reshape(load_count, 4 * face_width // block_width, block_width)


def spread(owned_part, slot_onehot, block_width):
    face_width = owned_part.shape[2] // 2
    own_sub = owned_part[:, :, :face_width]
    own_grp = owned_part[:, :, face_width:]
    from_sub = shifted(own_sub, "sub", 1)
    from_grp = shifted(own_grp, "grp", 1)
    directed = jnp.stack([from_sub[0], own_sub[0], from_grp[0], own_grp[0]], 0)
    return place_faces(directed, slot_onehot, block_width)


def collect(local_part, slot_onehot):
    load_count = local_part.shape[0]
    placed = local_part.reshape(load_count, 4, -1)
    directed = jnp.einsum("dk,lkf->dlf", slot_onehot, placed, precision=highest_precision)
    to_sub = shifted(directed[0][None], "sub", -1)
    to_grp = shifted(directed[2][None], "grp", -1)
    owned_sub = directed[1][None] + to_sub
    owned_grp = directed[3][None] + to_grp
    return jnp.concatenate([owned_sub, owned_grp], 2)


def condensed(vector, couple, dirichlet, face_matrix):
    count_of_blocks = vector.shape[1]
    block_width = vector.shape[2]
    paired = jnp.concatenate(
        [
            jnp.concatenate([vector, jnp.roll(vector, -(offset + 1), axis=1)], 2)
            for offset in range(3)
        ],
        1,
    )
    interior = jnp.einsum("lib,ibk->lik", paired, couple, precision=highest_precision)
    middle = jnp.einsum("lik,ikm->lim", interior, dirichlet, precision=highest_precision)
    solved = jnp.einsum("lim,ikm->lik", middle, dirichlet, precision=highest_precision)
    returned = jnp.einsum("lik,ibk->lib", solved, couple, precision=highest_precision)
    result = jnp.einsum("ljb,jbk->ljk", vector, face_matrix, precision=highest_precision)
    for offset in range(3):
        portion = returned[:, offset * count_of_blocks : (offset + 1) * count_of_blocks]
        result = (
            result
            + portion[:, :, :block_width]
            + jnp.roll(portion[:, :, block_width:], offset + 1, axis=1)
        )
    return result


def coarse_neighbors(initial_step, pattern, matrix):
    load_count, primal_count = initial_step.shape
    grp_count = lax.axis_size("grp")
    sub_count = lax.axis_size("sub")
    reach_count = 2 * REACH_SUBS + 1
    entry_sub = pattern // grp_count
    entry_grp = pattern % grp_count
    position = (entry_sub - lax.axis_index("sub") + REACH_SUBS) % sub_count
    column = lax.all_gather(initial_step[None], "grp", axis=0, tiled=True)
    pieces = []
    for place in range(reach_count):
        if place == REACH_SUBS:
            pieces.append(column)
        else:
            pieces.append(shifted(column, "sub", REACH_SUBS - place))
    window = jnp.stack(pieces, 0).reshape(-1, load_count, primal_count)
    slot_index = position * grp_count + entry_grp
    chooser = (slot_index[:, None] == jnp.arange(window.shape[0], dtype=jnp.int32)[None, :]).astype(
        jnp.float32
    )
    chosen = jnp.einsum("kj,jlc->klc", chooser, window, precision=highest_precision)
    return jnp.einsum("klc,kcd->ld", chosen, matrix, precision=highest_precision)


def precondition(
    local_copy, slot_onehot, neumann, block_ids, primal_rows, matrix, inverse, pattern
):
    halved = local_copy * 0.5
    neumann_step = jnp.einsum("ljb,jbk->ljk", halved, neumann, precision=highest_precision)
    local_solve = jnp.einsum("ljk,jmk->ljm", neumann_step, neumann, precision=highest_precision)
    selector = (block_ids[:, None] == jnp.arange(halved.shape[1], dtype=jnp.int32)[None, :]).astype(
        jnp.float32
    )
    picked = jnp.einsum("ljb,cj->lcb", halved, selector, precision=highest_precision)
    coarse_residual = jnp.einsum("lcb,cb->lc", picked, primal_rows, precision=highest_precision)
    initial_step = jnp.dot(coarse_residual, inverse, precision=highest_precision)
    adjacent_sum = coarse_neighbors(initial_step, pattern, matrix)
    coarse_correction = initial_step + jnp.dot(
        coarse_residual - adjacent_sum, inverse, precision=highest_precision
    )
    weighted = coarse_correction[:, :, None] * primal_rows[None]
    spread_back = jnp.einsum("lcb,cj->ljb", weighted, selector, precision=highest_precision)
    return collect(0.5 * (local_solve + spread_back), slot_onehot)


def shards(
    solution,
    residual,
    direction,
    residual_product,
    neighbor_slots,
    coupling,
    dirichlet_factor,
    face_block,
    neumann_factor,
    primal_block,
    primal_basis,
    coarse_matrix,
    coarse_block_inverse,
    coarse_pattern,
):
    slot_onehot = slot_table(neighbor_slots)
    block_width = face_block.shape[2]
    couple = coupling[0].astype(jnp.float32)
    dirichlet = dirichlet_factor[0].astype(jnp.float32)
    face_matrix = face_block[0].astype(jnp.float32)
    neumann = neumann_factor[0].astype(jnp.float32)
    primal_rows = primal_basis[0].astype(jnp.float32)
    direction_local = spread(direction, slot_onehot, block_width)
    image = collect(condensed(direction_local, couple, dirichlet, face_matrix), slot_onehot)
    curvature = lax.psum(jnp.sum(direction * image, axis=(0, 2)), ("sub", "grp"))
    step_length = residual_product / curvature
    new_residual = residual - step_length[None, :, None] * image
    new_local = spread(new_residual, slot_onehot, block_width)
    preconditioned = precondition(
        new_local,
        slot_onehot,
        neumann,
        primal_block[0],
        primal_rows,
        coarse_matrix[0],
        coarse_block_inverse[0],
        coarse_pattern[0],
    )
    new_product = lax.psum(jnp.sum(new_residual * preconditioned, axis=(0, 2)), ("sub", "grp"))
    new_solution = solution + step_length[None, :, None] * direction
    step_ratio = new_product / residual_product
    new_direction = preconditioned + step_ratio[None, :, None] * direction
    return (new_solution, new_residual, new_direction, new_product)


def solution(mesh):
    in_specs = (
        P(("sub", "grp"), None, None),
        P(("sub", "grp"), None, None),
        P(("sub", "grp"), None, None),
        P(),
        P(("sub", "grp"), None),
        P(("sub", "grp"), None, None, None),
        P(("sub", "grp"), None, None, None),
        P(("sub", "grp"), None, None, None),
        P(("sub", "grp"), None, None, None),
        P(("sub", "grp"), None),
        P(("sub", "grp"), None, None),
        P(("sub", "grp"), None, None, None),
        P(("sub", "grp"), None, None),
        P(("sub", "grp"), None),
    )
    out_specs = (
        P(("sub", "grp"), None, None),
        P(("sub", "grp"), None, None),
        P(("sub", "grp"), None, None),
        P(),
    )
    return jax.shard_map(shards, mesh=mesh, in_specs=in_specs, out_specs=out_specs, check_vma=False)
```

profile of v0, /device:TPU:0, one launch (start us, length us, event | category | flops | bytes accessed | tf_op | source)
XLA Modules:
  0.0 302.8 jit_solution(3611158063502701570)
XLA Ops:
  6.3 14.4 %collective-permute-done = f32[1,128,1024]{2,0,1:T(1,128)S(1)} collective-permute-done((f32[1,128,1024]{2,0,1:T(1,128)S(1)}, f32[1,128,1024]{2,0,1:T(1,128)S(1)}, u32[]{:S(2)}, u32[]{:S(2)}) %collective-permute-start) | collective-permute-done | bytes 524320 | tf_op jit(solution)/shard_map/ppermute | solution.py:13
  20.6 5.2 %fusion.45 = f32[128,4,1024]{2,1,0:T(4,128)} fusion(f32[1,128,1024]{2,0,1:T(1,128)S(1)} %copy.71, f32[1,128,1024]{2,0,1:T(1,128)S(1)} %collective-permute-done.1, f32[1,128,1024]{2,0,1:T(1,128)S(1)} %copy.70, f32[1,128,1024]{2,0,1:T(1,128)S(1)} %collective-permute-done, s32[4]{0:T(128)S(1)} %bitcast.127), kind=kOutput, calls=%fused_computation.46 | convolution fusion | flops 26738704 | bytes 4194320 | tf_op jit(solution)/shard_map/dk,dlf->lkf/dot_general | solution.py:25
  31.9 6.1 %maximum_maximum_fusion = f32[128,96,256]{2,1,0:T(8,128)} fusion(f32[128,3,128]{2,1,0:T(4,128)S(1)} %slice.143, f32[128,29,128]{2,1,0:T(8,128)S(1)} %slice.142, f32[128,32,128]{2,1,0:T(8,128)S(1)} %copy-done.2, f32[128,2,128]{2,1,0:T(2,128)S(1)} %slice.141, f32[128,30,128]{2,1,0:T(8,128)S(1)} %slice.140, f32[128,1,128]{2,1,0:T(1,128)S(1)} %slice.139, ...), kind=kLoop, calls=%fused_computation | loop fusion | flops 25165824 | bytes 20971520 | tf_op jit(solution)/shard_map/concatenate | solution.py:53
  37.9 21.7 %fusion = f32[96,128,128]{2,1,0:T(8,128)} fusion(f32[128,96,256]{2,1,0:T(8,128)} %maximum_maximum_fusion, bf16[1,96,256,128]{3,2,1,0:T(8,128)(2,1)} %param.19), kind=kOutput, calls=%fused_computation.1 | convolution fusion | flops 4831838208 | bytes 25165824 | tf_op jit(solution)/shard_map/lib,ibk->lik/dot_general | solution.py:60
  59.6 5.3 %fusion.11 = f32[96,128,128]{2,1,0:T(8,128)S(1)} fusion(f32[96,128,128]{2,1,0:T(8,128)} %fusion, bf16[1,96,128,128]{3,2,1,0:T(8,128)(2,1)S(1)} %copy-done), kind=kOutput, calls=%fused_computation.12 | convolution fusion | flops 2415919104 | bytes 15728640 | tf_op jit(solution)/shard_map/lik,ikm->lim/dot_general | solution.py:61
  64.9 8.5 %fusion.9 = f32[96,128,128]{2,1,0:T(8,128)} fusion(f32[96,128,128]{2,1,0:T(8,128)S(1)} %fusion.11, bf16[1,96,128,128]{3,2,1,0:T(8,128)(2,1)S(1)} %copy-done), kind=kOutput, calls=%fused_computation.10 | convolution fusion | flops 2415919104 | bytes 15728640 | tf_op jit(solution)/shard_map/lim,ikm->lik/dot_general | solution.py:62
  73.4 8.4 %fusion.15 = f32[128,96,256]{0,2,1:T(8,128)S(1)} fusion(bf16[1,96,256,128]{3,2,1,0:T(8,128)(2,1)} %param.19, f32[96,128,128]{2,1,0:T(8,128)} %fusion.9), kind=kOutput, calls=%fused_computation.16 | convolution fusion | flops 4831838208 | bytes 25165824 | tf_op jit(solution)/shard_map/lik,ibk->lib/dot_general | solution.py:63
  84.0 5.4 %fusion.24 = f32[128,32,128]{0,2,1:T(8,128)} fusion(f32[128,96,256]{0,2,1:T(8,128)S(1)} %fusion.15, f32[128,31,128]{0,2,1:T(8,128)S(1)} %slice.146, f32[128,1,128]{0,2,1:T(8,128)S(1)} %slice.145, f32[128,30,128]{0,2,1:T(8,128)S(1)} %slice.149, f32[128,2,128]{0,2,1:T(8,128)S(1)} %slice.148, f32[128,29,128]{0,2,1:T(8,128)S(1)} %slice.152, ...), kind=kOutput, calls=%fused_computation.22 | convolution fusion | flops 810024960 | bytes 17825792 | tf_op jit(solution)/shard_map/ljb,jbk->ljk/dot_general | solution.py:64
  92.7 3.7 %fusion.82 = f32[4,128,1024]{2,0,1:T(4,128)S(1)} fusion(f32[128,4,1024]{2,1,0:T(4,128)} %copy.44, s32[4]{0:T(128)S(1)} %bitcast.128), kind=kOutput, calls=%fused_computation.102 | convolution fusion | flops 25165840 | bytes 4194320 | tf_op jit(solution)/shard_map/dk,lkf->dlf/dot_general | solution.py:42
  100.0 11.2 %collective-permute-done.2 = f32[1,128,1024]{2,1,0:T(8,128)S(1)} collective-permute-done((f32[1,128,1024]{2,1,0:T(8,128)S(1)}, f32[1,128,1024]{2,1,0:T(8,128)S(1)}, u32[]{:S(2)}, u32[]{:S(2)}) %collective-permute-start.2) | collective-permute-done | bytes 524320 | tf_op jit(solution)/shard_map/ppermute | solution.py:13
  111.7 39.6 %psum.14 = f32[128]{0:T(128)S(1)} all-reduce(f32[128]{0:T(128)S(1)} %multiply_reduce_fusion.1), channel_id=1, replica_groups=mesh['sub'=8,'grp'=4] {'sub','grp'}, use_global_device_ids=true, to_apply=%region_1.2 | all-reduce | flops 128 | bytes 1024 | tf_op jit(solution)/shard_map/psum | solution.py:145
  155.2 13.2 %collective-permute-done.4 = f32[1,128,1024]{2,1,0:T(8,128)S(1)} collective-permute-done((f32[1,128,1024]{2,1,0:T(8,128)S(1)}, f32[1,128,1024]{2,1,0:T(8,128)S(1)}, u32[]{:S(2)}, u32[]{:S(2)}) %collective-permute-start.4) | collective-permute-done | bytes 524320 | tf_op jit(solution)/shard_map/ppermute | solution.py:13
  171.0 4.8 %multiply_bitcast_fusion = f32[128,4,1024]{2,1,0:T(4,128)} fusion(f32[4,128,1024]{2,1,0:T(8,128)S(1)} %pad_maximum_fusion, s32[4]{0:T(128)S(1)} %bitcast.129), kind=kOutput, calls=%fused_computation.45 | convolution fusion | flops 25690128 | bytes 4194320 | tf_op jit(solution)/shard_map/dk,dlf->lkf/dot_general | solution.py:25
  181.8 11.0 %fusion.2 = f32[128,1,128]{2,1,0:T(1,128)S(1)} fusion(f32[128,128,128]{2,0,1:T(8,128)S(1)} %fusion.66, bf16[128,128,1]{1,0,2:T(8,128)(2,1)S(1)} %bitcast.126), kind=kOutput, calls=%fused_computation.3 | convolution fusion | flops 25165824 | bytes 8486912 | tf_op jit(solution)/shard_map/lcb,cb->lc/dot_general | solution.py:109
  193.1 5.8 %all-gather = f32[512,128]{1,0:T(8,128)S(1)} all-gather(f32[128,128]{1,0:T(8,128)S(1)} %fusion.61), channel_id=2, replica_groups=mesh['sub'=8,'grp'=4] {'grp'}, dimensions={0}, use_global_device_ids=true | all-gather | bytes 327680 | tf_op jit(solution)/shard_map/all_gather | solution.py:83
  199.6 4.3 %collective-permute-start.8 = (f32[4,128,128]{2,1,0:T(8,128)S(1)}, f32[4,128,128]{2,1,0:T(8,128)S(1)}, u32[]{:S(2)}, u32[]{:S(2)}) collective-permute-start(f32[4,128,128]{2,1,0:T(8,128)S(1)} %bitcast.121), channel_id=1, source_target_pairs={{0,28},{4,0},{8,4},{12,8},{16,12},{20,16},{24,20},{28,24},{1,29},{... | collective-permute-start | bytes 786440 | tf_op jit(solution)/shard_map/ppermute | solution.py:13
  205.6 3.6 %fusion.37 = f32[32,128,128]{2,1,0:T(8,128)} fusion(f32[128,32,128]{2,1,0:T(8,128)S(1)} %mul.80, bf16[1,32,128,128]{3,2,1,0:T(8,128)(2,1)S(1)} %copy-done.9), kind=kOutput, calls=%fused_computation.38 | convolution fusion | flops 805306368 | bytes 5242880 | tf_op jit(solution)/shard_map/ljb,jbk->ljk/dot_general | solution.py:103
  210.0 3.6 %collective-permute-done.7 = f32[4,128,128]{2,1,0:T(8,128)S(1)} collective-permute-done((f32[4,128,128]{2,1,0:T(8,128)S(1)}, f32[4,128,128]{2,1,0:T(8,128)S(1)}, u32[]{:S(2)}, u32[]{:S(2)}) %collective-permute-start.7) | collective-permute-done | bytes 262176 | tf_op jit(solution)/shard_map/ppermute | solution.py:13
  213.9 6.6 %collective-permute-done.9 = f32[4,128,128]{2,1,0:T(8,128)S(1)} collective-permute-done((f32[4,128,128]{2,1,0:T(8,128)S(1)}, f32[4,128,128]{2,1,0:T(8,128)S(1)}, u32[]{:S(2)}, u32[]{:S(2)}) %collective-permute-start.9) | collective-permute-done | bytes 262176 | tf_op jit(solution)/shard_map/ppermute | solution.py:13
  223.5 5.3 %fusion.5 = f32[32,128,128]{2,0,1:T(8,128)} fusion(f32[128,128]{1,0:T(8,128)S(1)} %bitcast_convert_fusion, f32[128,128]{1,0:T(8,128)S(1)} %convolution_add_fusion, s32[128]{0:T(128)S(1)} %bitcast.132), kind=kOutput, calls=%fused_computation.6 | convolution fusion | flops 807407616 | bytes 2228736 | tf_op jit(solution)/shard_map/lcb,cj->ljb/dot_general | solution.py:116
  231.9 5.5 %add_multiply_fusion = f32[32,128,128]{1,2,0:T(8,128)} fusion(f32[32,128,128]{1,2,0:T(8,128)} %copy.51, f32[32,128,128]{2,1,0:T(8,128)S(1)} %copy-done.6, bf16[1,32,128,128]{3,2,1,0:T(8,128)(2,1)} %param.22), kind=kOutput, calls=%fused_computation.44 | convolution fusion | flops 806354944 | bytes 7340032 | tf_op jit(solution)/shard_map/ljk,jmk->ljm/dot_general | solution.py:104
  240.6 3.7 %fusion.80 = f32[4,128,1024]{2,0,1:T(4,128)S(1)} fusion(f32[128,4,1024]{2,1,0:T(4,128)} %copy.52, s32[4]{0:T(128)S(1)} %bitcast.130), kind=kOutput, calls=%fused_computation.101 | convolution fusion | flops 25165840 | bytes 4194320 | tf_op jit(solution)/shard_map/dk,lkf->dlf/dot_general | solution.py:42
  247.0 12.8 %collective-permute-done.10 = f32[1,128,1024]{2,1,0:T(8,128)S(1)} collective-permute-done((f32[1,128,1024]{2,1,0:T(8,128)S(1)}, f32[1,128,1024]{2,1,0:T(8,128)S(1)}, u32[]{:S(2)}, u32[]{:S(2)}) %collective-permute-start.10) | collective-permute-done | bytes 524320 | tf_op jit(solution)/shard_map/ppermute | solution.py:13
  260.9 38.0 %psum.15 = f32[128]{0:T(128)S(1)} all-reduce(f32[128]{0:T(128)S(1)} %multiply_reduce_fusion), channel_id=1, replica_groups=mesh['sub'=8,'grp'=4] {'sub','grp'}, use_global_device_ids=true, to_apply=%region_3.4 | all-reduce | flops 128 | bytes 1024 | tf_op jit(solution)/shard_map/psum | solution.py:159
  (111 shorter events, 53.8 us)
Async XLA Ops:
  0.6 59.0 %copy-start = (bf16[1,96,128,128]{3,2,1,0:T(8,128)(2,1)S(1)}, bf16[1,96,128,128]{3,2,1,0:T(8,128)(2,1)}, u32[]{:S(2)}) copy-start(bf16[1,96,128,128]{3,2,1,0:T(8,128)(2,1)} %param.20) | copy-start | bytes 9437188
  0.6 20.0 %copy-start.17 = (s32[1,4]{1,0:T(1,128)S(1)}, s32[1,4]{1,0:T(1,128)}, u32[]{:S(2)}) copy-start(s32[1,4]{1,0:T(1,128)} %param.18) | copy-start | bytes 52
  2.6 18.0 %collective-permute-start = (f32[1,128,1024]{2,0,1:T(1,128)S(1)}, f32[1,128,1024]{2,0,1:T(1,128)S(1)}, u32[]{:S(2)}, u32[]{:S(2)}) collective-permute-start(f32[1,128,1024]{2,0,1:T(1,128)S(1)} %copy.70), channel_id=1, source_target_pairs={{0,4},{4,8},{8,12},{12,16},{16,20},{20,24},{24,28},{28,0},{1,5},{5... | collective-permute-start | bytes 1572872 | tf_op jit(solution)/shard_map/ppermute | solution.py:13
  6.2 14.4 %collective-permute-start.1 = (f32[1,128,1024]{2,0,1:T(1,128)S(1)}, f32[1,128,1024]{2,0,1:T(1,128)S(1)}, u32[]{:S(2)}, u32[]{:S(2)}) collective-permute-start(f32[1,128,1024]{2,0,1:T(1,128)S(1)} %copy.71), channel_id=1, source_target_pairs={{0,1},{1,2},{2,3},{3,0},{4,5},{5,6},{6,7},{7,4},{8,9},{9,10},{10,1... | collective-permute-start | bytes 1572872 | tf_op jit(solution)/shard_map/ppermute | solution.py:13
  98.1 13.1 %collective-permute-start.2 = (f32[1,128,1024]{2,1,0:T(8,128)S(1)}, f32[1,128,1024]{2,1,0:T(8,128)S(1)}, u32[]{:S(2)}, u32[]{:S(2)}) collective-permute-start(f32[1,128,1024]{2,1,0:T(8,128)S(1)} %copy.73), channel_id=1, source_target_pairs={{0,28},{4,0},{8,4},{12,8},{16,12},{20,16},{24,20},{28,24},{1,29},{... | collective-permute-start | bytes 1572872 | tf_op jit(solution)/shard_map/ppermute | solution.py:13
  99.9 11.6 %copy-start.5 = (f32[1,128,2048]{2,1,0:T(8,128)S(1)}, f32[1,128,2048]{2,1,0:T(8,128)}, u32[]{:S(2)}) copy-start(f32[1,128,2048]{2,1,0:T(8,128)} %param.16) | copy-start | bytes 3145732
  100.0 11.4 %collective-permute-start.3 = (f32[1,128,1024]{2,1,0:T(8,128)S(1)}, f32[1,128,1024]{2,1,0:T(8,128)S(1)}, u32[]{:S(2)}, u32[]{:S(2)}) collective-permute-start(f32[1,128,1024]{2,1,0:T(8,128)S(1)} %copy.75), channel_id=1, source_target_pairs={{0,3},{1,0},{2,1},{3,2},{4,7},{5,4},{6,5},{7,6},{8,11},{9,8},{10,9... | collective-permute-start | bytes 1572872 | tf_op jit(solution)/shard_map/ppermute | solution.py:13
  111.3 39.9 %copy-start.20 = (f32[128]{0:T(128)S(1)}, f32[128]{0:T(128)}, u32[]{:S(2)}) copy-start(f32[128]{0:T(128)} %param.17) | copy-start | bytes 1540
  151.3 3.9 %copy-start.19 = (s32[1,9]{1,0:T(1,128)S(1)}, s32[1,9]{1,0:T(1,128)}, u32[]{:S(2)}) copy-start(s32[1,9]{1,0:T(1,128)} %param.27) | copy-start | bytes 112
  151.3 3.9 %copy-start.15 = (bf16[1,128,128]{2,1,0:T(8,128)(2,1)S(1)}, bf16[1,128,128]{2,1,0:T(8,128)(2,1)}, u32[]{:S(2)}) copy-start(bf16[1,128,128]{2,1,0:T(8,128)(2,1)} %param.24) | copy-start | bytes 98308
  152.7 107.4 %copy-start.4 = (f32[1,128,2048]{2,1,0:T(8,128)}, f32[1,128,2048]{2,1,0:T(8,128)S(1)}, u32[]{:S(2)}) copy-start(f32[1,128,2048]{2,1,0:T(8,128)S(1)} %multiply_subtract_fusion) | copy-start | bytes 3145732
  152.8 15.6 %copy-start.10 = (f32[1,128,1024]{2,1,0:T(8,128)}, f32[1,128,1024]{2,1,0:T(8,128)S(1)}, u32[]{:S(2)}) copy-start(f32[1,128,1024]{2,1,0:T(8,128)S(1)} %get-tuple-element.18) | copy-start | bytes 1572868
  152.8 15.6 %copy-start.11 = (f32[1,128,1024]{2,1,0:T(8,128)}, f32[1,128,1024]{2,1,0:T(8,128)S(1)}, u32[]{:S(2)}) copy-start(f32[1,128,1024]{2,1,0:T(8,128)S(1)} %get-tuple-element.19) | copy-start | bytes 1572868
  152.8 15.6 %collective-permute-start.4 = (f32[1,128,1024]{2,1,0:T(8,128)S(1)}, f32[1,128,1024]{2,1,0:T(8,128)S(1)}, u32[]{:S(2)}, u32[]{:S(2)}) collective-permute-start(f32[1,128,1024]{2,1,0:T(8,128)S(1)} %get-tuple-element.18), channel_id=1, source_target_pairs={{0,4},{4,8},{8,12},{12,16},{16,20},{20,24},{24,28},{28,0},{1,5},{5... | collective-permute-start | bytes 1572872 | tf_op jit(solution)/shard_map/ppermute | solution.py:13
  155.2 14.1 %collective-permute-start.5 = (f32[1,128,1024]{2,1,0:T(8,128)S(1)}, f32[1,128,1024]{2,1,0:T(8,128)}, u32[]{:S(2)}, u32[]{:S(2)}) collective-permute-start(f32[1,128,1024]{2,1,0:T(8,128)S(1)} %get-tuple-element.19), channel_id=1, source_target_pairs={{0,1},{1,2},{2,3},{3,0},{4,5},{5,6},{6,7},{7,4},{8,9},{9,10},{10,1... | collective-permute-start | bytes 1572872 | tf_op jit(solution)/shard_map/ppermute | solution.py:13
  181.8 11.0 %copy-start.16 = (f32[1,128,128]{2,1,0:T(8,128)S(1)}, f32[1,128,128]{2,1,0:T(8,128)}, u32[]{:S(2)}) copy-start(f32[1,128,128]{2,1,0:T(8,128)} %param.26) | copy-start | bytes 196612
  181.8 23.8 %copy-start.9 = (bf16[1,32,128,128]{3,2,1,0:T(8,128)(2,1)S(1)}, bf16[1,32,128,128]{3,2,1,0:T(8,128)(2,1)}, u32[]{:S(2)}) copy-start(bf16[1,32,128,128]{3,2,1,0:T(8,128)(2,1)} %param.22) | copy-start | bytes 3145732
  198.9 11.1 %collective-permute-start.6 = (f32[4,128,128]{2,1,0:T(8,128)S(1)}, f32[4,128,128]{2,1,0:T(8,128)S(1)}, u32[]{:S(2)}, u32[]{:S(2)}) collective-permute-start(f32[4,128,128]{2,1,0:T(8,128)S(1)} %bitcast.119), channel_id=1, source_target_pairs={{0,8},{4,12},{8,16},{12,20},{16,24},{20,28},{24,0},{28,4},{1,9},{5... | collective-permute-start | bytes 786440 | tf_op jit(solution)/shard_map/ppermute | solution.py:13
  199.2 14.4 %collective-permute-start.7 = (f32[4,128,128]{2,1,0:T(8,128)S(1)}, f32[4,128,128]{2,1,0:T(8,128)S(1)}, u32[]{:S(2)}, u32[]{:S(2)}) collective-permute-start(f32[4,128,128]{2,1,0:T(8,128)S(1)} %bitcast.120), channel_id=1, source_target_pairs={{0,4},{4,8},{8,12},{12,16},{16,20},{20,24},{24,28},{28,0},{1,5},{5... | collective-permute-start | bytes 786440 | tf_op jit(solution)/shard_map/ppermute | solution.py:13
  199.6 14.3 %collective-permute-start.8 = (f32[4,128,128]{2,1,0:T(8,128)S(1)}, f32[4,128,128]{2,1,0:T(8,128)S(1)}, u32[]{:S(2)}, u32[]{:S(2)}) collective-permute-start(f32[4,128,128]{2,1,0:T(8,128)S(1)} %bitcast.121), channel_id=1, source_target_pairs={{0,28},{4,0},{8,4},{12,8},{16,12},{20,16},{24,20},{28,24},{1,29},{... | collective-permute-start | bytes 786440 | tf_op jit(solution)/shard_map/ppermute | solution.py:13
  203.9 16.6 %collective-permute-start.9 = (f32[4,128,128]{2,1,0:T(8,128)S(1)}, f32[4,128,128]{2,1,0:T(8,128)S(1)}, u32[]{:S(2)}, u32[]{:S(2)}) collective-permute-start(f32[4,128,128]{2,1,0:T(8,128)S(1)} %bitcast.122), channel_id=1, source_target_pairs={{0,24},{4,28},{8,0},{12,4},{16,8},{20,12},{24,16},{28,20},{1,25},{... | collective-permute-start | bytes 786440 | tf_op jit(solution)/shard_map/ppermute | solution.py:13
  213.6 8.4 %copy-start.13 = (f32[1,9,128,128]{3,2,1,0:T(8,128)S(1)}, f32[1,9,128,128]{3,2,1,0:T(8,128)}, u32[]{:S(2)}) copy-start(f32[1,9,128,128]{3,2,1,0:T(8,128)} %param.25) | copy-start | bytes 1769476
  245.9 13.9 %collective-permute-start.10 = (f32[1,128,1024]{2,1,0:T(8,128)S(1)}, f32[1,128,1024]{2,1,0:T(8,128)S(1)}, u32[]{:S(2)}, u32[]{:S(2)}) collective-permute-start(f32[1,128,1024]{2,1,0:T(8,128)S(1)} %copy.77), channel_id=1, source_target_pairs={{0,28},{4,0},{8,4},{12,8},{16,12},{20,16},{24,20},{28,24},{1,29},{... | collective-permute-start | bytes 1572872 | tf_op jit(solution)/shard_map/ppermute | solution.py:13
  246.2 13.8 %collective-permute-start.11 = (f32[1,128,1024]{2,1,0:T(8,128)S(1)}, f32[1,128,1024]{2,1,0:T(8,128)S(1)}, u32[]{:S(2)}, u32[]{:S(2)}) collective-permute-start(f32[1,128,1024]{2,1,0:T(8,128)S(1)} %copy.79), channel_id=1, source_target_pairs={{0,3},{1,0},{2,1},{3,2},{4,7},{5,4},{6,5},{7,6},{8,11},{9,8},{10,9... | collective-permute-start | bytes 1572872 | tf_op jit(solution)/shard_map/ppermute | solution.py:13
  (10 other events, 20.9 us)
where the time goes:
time: 308 us; the launch traced here: 303 us
  matrix products  98.6 us (32%)
  blocking collectives  83.4 us (27%)
  waiting for transfers between devices  62.8 us (20%)
  local copies, waits for them, and re-layouts  27.9 us (9%)
  starting transfers between devices  14.9 us (5%)
  other arithmetic  13.7 us (4%)
    ppermute x12, waiting for transfers between devices, shifted(): return lax.ppermute(value, axis, pairs)  62.8 us
    psum x1, blocking collectives, shards(): lax.psum(jnp.sum(direction * image, axis=(0, 2)), ('sub', 'grp'))  39.6 us
    psum x1, blocking collectives, shards(): lax.psum(jnp.sum(new_residual * preconditioned, axis=(0, 2)), ('sub', 'gr...  38 us
    dot_general x1, matrix products, condensed(): jnp.einsum('lib,ibk->lik', paired, couple, precision=highest_precision)  21.7 us
    ppermute x12, starting transfers between devices, shifted(): return lax.ppermute(value, axis, pairs)  14.9 us
    dot_general x1, matrix products, precondition(): jnp.einsum('lcb,cb->lc', picked, primal_rows, precision=highest_precision)  11 us
    dot_general x2, matrix products, place_faces(): jnp.einsum('dk,dlf->lkf', slot_onehot, directed, precision=highest_precis...  9.93 us
    dot_general x1, matrix products, condensed(): jnp.einsum('lim,ikm->lik', middle, dirichlet, precision=highest_precision)  8.47 us
  transfers between devices with their start and end apart: 12, of which 8 were waited for; matrix products, arithmetic and copies ran while one was open for 2% of the time, Pallas kernels for 0%

commit v1 on v0

--- a/solution.py
+++ b/solution.py
@@ -142,7 +142,7 @@
     primal_rows = primal_basis[0].astype(jnp.float32)
     direction_local = spread(direction, slot_onehot, block_width)
     image = collect(condensed(direction_local, couple, dirichlet, face_matrix), slot_onehot)
-    curvature = lax.psum(jnp.sum(direction * image, axis=(0, 2)), ("sub", "grp"))
+    curvature = lax.psum(lax.psum(jnp.sum(direction * image, axis=(0, 2)), "grp"), "sub")
     step_length = residual_product / curvature
     new_residual = residual - step_length[None, :, None] * image
     new_local = spread(new_residual, slot_onehot, block_width)

time: 308 us -> 292 us (0.948)
  blocking collectives: 83.4 us -> 74.3 us
  waiting for transfers between devices: 62.8 us -> 56.7 us
    psum x1 -> x2, blocking collectives: 39.6 us -> 26.9 us  [the longest x1 21.2 us: shards(): lax.psum(lax.psum(jnp.sum(direction * image, axis=(0, 2)), 'grp'), 'sub')]
    ppermute x12, waiting for transfers between devices: 62.8 us -> 56.7 us  [shifted(): return lax.ppermute(value, axis, pairs)]
    psum x1, blocking collectives: 38 us -> 41.6 us  [shards(): lax.psum(jnp.sum(new_residual * preconditioned, axis=(0, 2)), ('sub', 'gr...]
where the time goes in v1:
time: 292 us; the launch traced here: 287 us
  matrix products  98.7 us (34%)
  blocking collectives  74.3 us (25%)
  waiting for transfers between devices  56.7 us (19%)
  local copies, waits for them, and re-layouts  27.9 us (10%)
  starting transfers between devices  13.9 us (5%)
  other arithmetic  13.7 us (5%)
    ppermute x12, waiting for transfers between devices, shifted(): return lax.ppermute(value, axis, pairs)  56.7 us
    psum x1, blocking collectives, shards(): lax.psum(jnp.sum(new_residual * preconditioned, axis=(0, 2)), ('sub', 'gr...  41.6 us
    dot_general x1, matrix products, condensed(): jnp.einsum('lib,ibk->lik', paired, couple, precision=highest_precision)  21.7 us
    psum x1, blocking collectives, shards(): lax.psum(lax.psum(jnp.sum(direction * image, axis=(0, 2)), 'grp'), 'sub')  21.2 us
    ppermute x12, starting transfers between devices, shifted(): return lax.ppermute(value, axis, pairs)  13.9 us
    dot_general x1, matrix products, precondition(): jnp.einsum('lcb,cb->lc', picked, primal_rows, precision=highest_precision)  11 us
    dot_general x2, matrix products, place_faces(): jnp.einsum('dk,dlf->lkf', slot_onehot, directed, precision=highest_precis...  9.95 us
    dot_general x1, matrix products, condensed(): jnp.einsum('lim,ikm->lik', middle, dirichlet, precision=highest_precision)  8.5 us
  transfers between devices with their start and end apart: 12, of which 8 were waited for; matrix products, arithmetic and copies ran while one was open for 2% of the time, Pallas kernels for 0%

profile of v1, /device:TPU:0, one launch (start us, length us, event | category | flops | bytes accessed | tf_op | source)
XLA Modules:
  0.0 286.8 jit_solution(5397140383038634646)
XLA Ops:
  6.3 14.4 %collective-permute-done = f32[1,128,1024]{2,0,1:T(1,128)S(1)} collective-permute-done((f32[1,128,1024]{2,0,1:T(1,128)S(1)}, f32[1,128,1024]{2,0,1:T(1,128)S(1)}, u32[]{:S(2)}, u32[]{:S(2)}) %collective-permute-start) | collective-permute-done | bytes 524320 | tf_op jit(solution)/shard_map/ppermute | solution.py:13
  20.6 5.2 %fusion.45 = f32[128,4,1024]{2,1,0:T(4,128)} fusion(f32[1,128,1024]{2,0,1:T(1,128)S(1)} %copy.71, f32[1,128,1024]{2,0,1:T(1,128)S(1)} %collective-permute-done.1, f32[1,128,1024]{2,0,1:T(1,128)S(1)} %copy.70, f32[1,128,1024]{2,0,1:T(1,128)S(1)} %collective-permute-done, s32[4]{0:T(128)S(1)} %bitcast.127), kind=kOutput, calls=%fused_computation.46 | convolution fusion | flops 26738704 | bytes 4194320 | tf_op jit(solution)/shard_map/dk,dlf->lkf/dot_general | solution.py:25
  31.9 6.1 %maximum_maximum_fusion = f32[128,96,256]{2,1,0:T(8,128)} fusion(f32[128,3,128]{2,1,0:T(4,128)S(1)} %slice.143, f32[128,29,128]{2,1,0:T(8,128)S(1)} %slice.142, f32[128,32,128]{2,1,0:T(8,128)S(1)} %copy-done.2, f32[128,2,128]{2,1,0:T(2,128)S(1)} %slice.141, f32[128,30,128]{2,1,0:T(8,128)S(1)} %slice.140, f32[128,1,128]{2,1,0:T(1,128)S(1)} %slice.139, ...), kind=kLoop, calls=%fused_computation | loop fusion | flops 25165824 | bytes 20971520 | tf_op jit(solution)/shard_map/concatenate | solution.py:53
  38.0 21.7 %fusion = f32[96,128,128]{2,1,0:T(8,128)} fusion(f32[128,96,256]{2,1,0:T(8,128)} %maximum_maximum_fusion, bf16[1,96,256,128]{3,2,1,0:T(8,128)(2,1)} %param.19), kind=kOutput, calls=%fused_computation.1 | convolution fusion | flops 4831838208 | bytes 25165824 | tf_op jit(solution)/shard_map/lib,ibk->lik/dot_general | solution.py:60
  59.7 5.3 %fusion.11 = f32[96,128,128]{2,1,0:T(8,128)S(1)} fusion(f32[96,128,128]{2,1,0:T(8,128)} %fusion, bf16[1,96,128,128]{3,2,1,0:T(8,128)(2,1)S(1)} %copy-done), kind=kOutput, calls=%fused_computation.12 | convolution fusion | flops 2415919104 | bytes 15728640 | tf_op jit(solution)/shard_map/lik,ikm->lim/dot_general | solution.py:61
  65.0 8.5 %fusion.9 = f32[96,128,128]{2,1,0:T(8,128)} fusion(f32[96,128,128]{2,1,0:T(8,128)S(1)} %fusion.11, bf16[1,96,128,128]{3,2,1,0:T(8,128)(2,1)S(1)} %copy-done), kind=kOutput, calls=%fused_computation.10 | convolution fusion | flops 2415919104 | bytes 15728640 | tf_op jit(solution)/shard_map/lim,ikm->lik/dot_general | solution.py:62
  73.5 8.4 %fusion.15 = f32[128,96,256]{0,2,1:T(8,128)S(1)} fusion(bf16[1,96,256,128]{3,2,1,0:T(8,128)(2,1)} %param.19, f32[96,128,128]{2,1,0:T(8,128)} %fusion.9), kind=kOutput, calls=%fused_computation.16 | convolution fusion | flops 4831838208 | bytes 25165824 | tf_op jit(solution)/shard_map/lik,ibk->lib/dot_general | solution.py:63
  84.1 5.5 %fusion.24 = f32[128,32,128]{0,2,1:T(8,128)} fusion(f32[128,96,256]{0,2,1:T(8,128)S(1)} %fusion.15, f32[128,31,128]{0,2,1:T(8,128)S(1)} %slice.146, f32[128,1,128]{0,2,1:T(8,128)S(1)} %slice.145, f32[128,30,128]{0,2,1:T(8,128)S(1)} %slice.149, f32[128,2,128]{0,2,1:T(8,128)S(1)} %slice.148, f32[128,29,128]{0,2,1:T(8,128)S(1)} %slice.152, ...), kind=kOutput, calls=%fused_computation.22 | convolution fusion | flops 810024960 | bytes 17825792 | tf_op jit(solution)/shard_map/ljb,jbk->ljk/dot_general | solution.py:64
  92.8 3.7 %fusion.82 = f32[4,128,1024]{2,0,1:T(4,128)S(1)} fusion(f32[128,4,1024]{2,1,0:T(4,128)} %copy.44, s32[4]{0:T(128)S(1)} %bitcast.128), kind=kOutput, calls=%fused_computation.102 | convolution fusion | flops 25165840 | bytes 4194320 | tf_op jit(solution)/shard_map/dk,lkf->dlf/dot_general | solution.py:42
  100.1 11.2 %collective-permute-done.2 = f32[1,128,1024]{2,1,0:T(8,128)S(1)} collective-permute-done((f32[1,128,1024]{2,1,0:T(8,128)S(1)}, f32[1,128,1024]{2,1,0:T(8,128)S(1)}, u32[]{:S(2)}, u32[]{:S(2)}) %collective-permute-start.2) | collective-permute-done | bytes 524320 | tf_op jit(solution)/shard_map/ppermute | solution.py:13
  111.8 5.7 %psum.21 = f32[128]{0:T(128)S(1)} all-reduce(f32[128]{0:T(128)S(1)} %multiply_reduce_fusion.1), channel_id=1, replica_groups=mesh['sub'=8,'grp'=4] {'grp'}, use_global_device_ids=true, to_apply=%region_1.2 | all-reduce | flops 128 | bytes 1024 | tf_op jit(solution)/shard_map/psum | solution.py:145
  117.5 21.2 %psum.22 = f32[128]{0:T(128)S(1)} all-reduce(f32[128]{0:T(128)S(1)} %psum.21), channel_id=1, replica_groups=mesh['sub'=8,'grp'=4] {'sub'}, use_global_device_ids=true, to_apply=%region_2.3 | all-reduce | flops 128 | bytes 1024 | tf_op jit(solution)/shard_map/psum | solution.py:145
  140.5 12.5 %collective-permute-done.4 = f32[1,128,1024]{2,1,0:T(8,128)S(1)} collective-permute-done((f32[1,128,1024]{2,1,0:T(8,128)S(1)}, f32[1,128,1024]{2,1,0:T(8,128)S(1)}, u32[]{:S(2)}, u32[]{:S(2)}) %collective-permute-start.4) | collective-permute-done | bytes 524320 | tf_op jit(solution)/shard_map/ppermute | solution.py:13
  155.6 4.8 %multiply_bitcast_fusion = f32[128,4,1024]{2,1,0:T(4,128)} fusion(f32[4,128,1024]{2,1,0:T(8,128)S(1)} %pad_maximum_fusion, s32[4]{0:T(128)S(1)} %bitcast.129), kind=kOutput, calls=%fused_computation.45 | convolution fusion | flops 25690128 | bytes 4194320 | tf_op jit(solution)/shard_map/dk,dlf->lkf/dot_general | solution.py:25
  166.4 11.0 %fusion.2 = f32[128,1,128]{2,1,0:T(1,128)S(1)} fusion(f32[128,128,128]{2,0,1:T(8,128)S(1)} %fusion.66, bf16[128,128,1]{1,0,2:T(8,128)(2,1)S(1)} %bitcast.126), kind=kOutput, calls=%fused_computation.3 | convolution fusion | flops 25165824 | bytes 8486912 | tf_op jit(solution)/shard_map/lcb,cb->lc/dot_general | solution.py:109
  177.7 5.8 %all-gather = f32[512,128]{1,0:T(8,128)S(1)} all-gather(f32[128,128]{1,0:T(8,128)S(1)} %fusion.61), channel_id=2, replica_groups=mesh['sub'=8,'grp'=4] {'grp'}, dimensions={0}, use_global_device_ids=true | all-gather | bytes 327680 | tf_op jit(solution)/shard_map/all_gather | solution.py:83
  183.5 4.7 %collective-permute-start.8 = (f32[4,128,128]{2,1,0:T(8,128)S(1)}, f32[4,128,128]{2,1,0:T(8,128)S(1)}, u32[]{:S(2)}, u32[]{:S(2)}) collective-permute-start(f32[4,128,128]{2,1,0:T(8,128)S(1)} %bitcast.121), channel_id=1, source_target_pairs={{0,28},{4,0},{8,4},{12,8},{16,12},{20,16},{24,20},{28,24},{1,29},{... | collective-permute-start | bytes 786440 | tf_op jit(solution)/shard_map/ppermute | solution.py:13
  190.2 3.6 %fusion.37 = f32[32,128,128]{2,1,0:T(8,128)} fusion(f32[128,32,128]{2,1,0:T(8,128)S(1)} %mul.80, bf16[1,32,128,128]{3,2,1,0:T(8,128)(2,1)S(1)} %copy-done.9), kind=kOutput, calls=%fused_computation.38 | convolution fusion | flops 805306368 | bytes 5242880 | tf_op jit(solution)/shard_map/ljb,jbk->ljk/dot_general | solution.py:103
  204.0 5.4 %fusion.5 = f32[32,128,128]{2,0,1:T(8,128)} fusion(f32[128,128]{1,0:T(8,128)S(1)} %bitcast_convert_fusion, f32[128,128]{1,0:T(8,128)S(1)} %convolution_add_fusion, s32[128]{0:T(128)S(1)} %bitcast.132), kind=kOutput, calls=%fused_computation.6 | convolution fusion | flops 807407616 | bytes 2228736 | tf_op jit(solution)/shard_map/lcb,cj->ljb/dot_general | solution.py:116
  212.4 5.5 %add_multiply_fusion = f32[32,128,128]{1,2,0:T(8,128)} fusion(f32[32,128,128]{1,2,0:T(8,128)} %copy.51, f32[32,128,128]{2,1,0:T(8,128)S(1)} %copy-done.6, bf16[1,32,128,128]{3,2,1,0:T(8,128)(2,1)} %param.22), kind=kOutput, calls=%fused_computation.44 | convolution fusion | flops 806354944 | bytes 7340032 | tf_op jit(solution)/shard_map/ljk,jmk->ljm/dot_general | solution.py:104
  221.1 3.7 %fusion.80 = f32[4,128,1024]{2,0,1:T(4,128)S(1)} fusion(f32[128,4,1024]{2,1,0:T(4,128)} %copy.52, s32[4]{0:T(128)S(1)} %bitcast.130), kind=kOutput, calls=%fused_computation.101 | convolution fusion | flops 25165840 | bytes 4194320 | tf_op jit(solution)/shard_map/dk,lkf->dlf/dot_general | solution.py:42
  228.6 11.6 %collective-permute-done.10 = f32[1,128,1024]{2,1,0:T(8,128)S(1)} collective-permute-done((f32[1,128,1024]{2,1,0:T(8,128)S(1)}, f32[1,128,1024]{2,1,0:T(8,128)S(1)}, u32[]{:S(2)}, u32[]{:S(2)}) %collective-permute-start.10) | collective-permute-done | bytes 524320 | tf_op jit(solution)/shard_map/ppermute | solution.py:13
  241.3 41.6 %psum.23 = f32[128]{0:T(128)S(1)} all-reduce(f32[128]{0:T(128)S(1)} %multiply_reduce_fusion), channel_id=1, replica_groups=mesh['sub'=8,'grp'=4] {'sub','grp'}, use_global_device_ids=true, to_apply=%region_4.5 | all-reduce | flops 128 | bytes 1024 | tf_op jit(solution)/shard_map/psum | solution.py:159
  283.0 3.6 %multiply_add_fusion = (f32[1,128,2048]{2,1,0:T(8,128)}, f32[1,128,2048]{2,1,0:T(8,128)}) fusion(f32[1,128,2048]{2,1,0:T(8,128)} %param.16, f32[1,128,1024]{2,1,0:T(8,128)} %copy-done.8, f32[1,128,1024]{2,1,0:T(8,128)} %copy-done.7, f32[128]{0:T(128)S(1)} %div.23, f32[1,128,2048]{2,1,0:T(8,128)} %param.14, f32[128]{0:T(128)S(1)} %div.18), kind=kLoop, calls=%fused_computation.57 | loop fusion | flops 1310720 | bytes 5243904 | tf_op jit(solution)/shard_map/add | solution.py:162
  (112 shorter events, 54.9 us)
Async XLA Ops:
  0.6 59.0 %copy-start = (bf16[1,96,128,128]{3,2,1,0:T(8,128)(2,1)S(1)}, bf16[1,96,128,128]{3,2,1,0:T(8,128)(2,1)}, u32[]{:S(2)}) copy-start(bf16[1,96,128,128]{3,2,1,0:T(8,128)(2,1)} %param.20) | copy-start | bytes 9437188
  0.6 20.0 %copy-start.17 = (s32[1,4]{1,0:T(1,128)S(1)}, s32[1,4]{1,0:T(1,128)}, u32[]{:S(2)}) copy-start(s32[1,4]{1,0:T(1,128)} %param.18) | copy-start | bytes 52
  2.6 18.0 %collective-permute-start = (f32[1,128,1024]{2,0,1:T(1,128)S(1)}, f32[1,128,1024]{2,0,1:T(1,128)S(1)}, u32[]{:S(2)}, u32[]{:S(2)}) collective-permute-start(f32[1,128,1024]{2,0,1:T(1,128)S(1)} %copy.70), channel_id=1, source_target_pairs={{0,4},{4,8},{8,12},{12,16},{16,20},{20,24},{24,28},{28,0},{1,5},{5... | collective-permute-start | bytes 1572872 | tf_op jit(solution)/shard_map/ppermute | solution.py:13
  6.2 14.4 %collective-permute-start.1 = (f32[1,128,1024]{2,0,1:T(1,128)S(1)}, f32[1,128,1024]{2,0,1:T(1,128)S(1)}, u32[]{:S(2)}, u32[]{:S(2)}) collective-permute-start(f32[1,128,1024]{2,0,1:T(1,128)S(1)} %copy.71), channel_id=1, source_target_pairs={{0,1},{1,2},{2,3},{3,0},{4,5},{5,6},{6,7},{7,4},{8,9},{9,10},{10,1... | collective-permute-start | bytes 1572872 | tf_op jit(solution)/shard_map/ppermute | solution.py:13
  98.2 13.2 %collective-permute-start.2 = (f32[1,128,1024]{2,1,0:T(8,128)S(1)}, f32[1,128,1024]{2,1,0:T(8,128)S(1)}, u32[]{:S(2)}, u32[]{:S(2)}) collective-permute-start(f32[1,128,1024]{2,1,0:T(8,128)S(1)} %copy.73), channel_id=1, source_target_pairs={{0,28},{4,0},{8,4},{12,8},{16,12},{20,16},{24,20},{28,24},{1,29},{... | collective-permute-start | bytes 1572872 | tf_op jit(solution)/shard_map/ppermute | solution.py:13
  100.0 11.7 %copy-start.5 = (f32[1,128,2048]{2,1,0:T(8,128)S(1)}, f32[1,128,2048]{2,1,0:T(8,128)}, u32[]{:S(2)}) copy-start(f32[1,128,2048]{2,1,0:T(8,128)} %param.16) | copy-start | bytes 3145732
  100.1 11.4 %collective-permute-start.3 = (f32[1,128,1024]{2,1,0:T(8,128)S(1)}, f32[1,128,1024]{2,1,0:T(8,128)S(1)}, u32[]{:S(2)}, u32[]{:S(2)}) collective-permute-start(f32[1,128,1024]{2,1,0:T(8,128)S(1)} %copy.75), channel_id=1, source_target_pairs={{0,3},{1,0},{2,1},{3,2},{4,7},{5,4},{6,5},{7,6},{8,11},{9,8},{10,9... | collective-permute-start | bytes 1572872 | tf_op jit(solution)/shard_map/ppermute | solution.py:13
  111.5 27.3 %copy-start.20 = (f32[128]{0:T(128)S(1)}, f32[128]{0:T(128)}, u32[]{:S(2)}) copy-start(f32[128]{0:T(128)} %param.17) | copy-start | bytes 1540
  140.1 100.3 %copy-start.4 = (f32[1,128,2048]{2,1,0:T(8,128)}, f32[1,128,2048]{2,1,0:T(8,128)S(1)}, u32[]{:S(2)}) copy-start(f32[1,128,2048]{2,1,0:T(8,128)S(1)} %multiply_subtract_fusion) | copy-start | bytes 3145732
  140.3 12.7 %copy-start.10 = (f32[1,128,1024]{2,1,0:T(8,128)}, f32[1,128,1024]{2,1,0:T(8,128)S(1)}, u32[]{:S(2)}) copy-start(f32[1,128,1024]{2,1,0:T(8,128)S(1)} %get-tuple-element.18) | copy-start | bytes 1572868
  140.3 12.7 %copy-start.11 = (f32[1,128,1024]{2,1,0:T(8,128)}, f32[1,128,1024]{2,1,0:T(8,128)S(1)}, u32[]{:S(2)}) copy-start(f32[1,128,1024]{2,1,0:T(8,128)S(1)} %get-tuple-element.19) | copy-start | bytes 1572868
  140.3 12.7 %collective-permute-start.4 = (f32[1,128,1024]{2,1,0:T(8,128)S(1)}, f32[1,128,1024]{2,1,0:T(8,128)S(1)}, u32[]{:S(2)}, u32[]{:S(2)}) collective-permute-start(f32[1,128,1024]{2,1,0:T(8,128)S(1)} %get-tuple-element.18), channel_id=1, source_target_pairs={{0,4},{4,8},{8,12},{12,16},{16,20},{20,24},{24,28},{28,0},{1,5},{5... | collective-permute-start | bytes 1572872 | tf_op jit(solution)/shard_map/ppermute | solution.py:13
  140.4 13.4 %collective-permute-start.5 = (f32[1,128,1024]{2,1,0:T(8,128)S(1)}, f32[1,128,1024]{2,1,0:T(8,128)}, u32[]{:S(2)}, u32[]{:S(2)}) collective-permute-start(f32[1,128,1024]{2,1,0:T(8,128)S(1)} %get-tuple-element.19), channel_id=1, source_target_pairs={{0,1},{1,2},{2,3},{3,0},{4,5},{5,6},{6,7},{7,4},{8,9},{9,10},{10,1... | collective-permute-start | bytes 1572872 | tf_op jit(solution)/shard_map/ppermute | solution.py:13
  166.4 11.0 %copy-start.16 = (f32[1,128,128]{2,1,0:T(8,128)S(1)}, f32[1,128,128]{2,1,0:T(8,128)}, u32[]{:S(2)}) copy-start(f32[1,128,128]{2,1,0:T(8,128)} %param.26) | copy-start | bytes 196612
  166.4 23.8 %copy-start.9 = (bf16[1,32,128,128]{3,2,1,0:T(8,128)(2,1)S(1)}, bf16[1,32,128,128]{3,2,1,0:T(8,128)(2,1)}, u32[]{:S(2)}) copy-start(bf16[1,32,128,128]{3,2,1,0:T(8,128)(2,1)} %param.22) | copy-start | bytes 3145732
  183.5 11.0 %collective-permute-start.6 = (f32[4,128,128]{2,1,0:T(8,128)S(1)}, f32[4,128,128]{2,1,0:T(8,128)S(1)}, u32[]{:S(2)}, u32[]{:S(2)}) collective-permute-start(f32[4,128,128]{2,1,0:T(8,128)S(1)} %bitcast.119), channel_id=1, source_target_pairs={{0,8},{4,12},{8,16},{12,20},{16,24},{20,28},{24,0},{28,4},{1,9},{5... | collective-permute-start | bytes 786440 | tf_op jit(solution)/shard_map/ppermute | solution.py:13
  183.5 13.7 %collective-permute-start.7 = (f32[4,128,128]{2,1,0:T(8,128)S(1)}, f32[4,128,128]{2,1,0:T(8,128)S(1)}, u32[]{:S(2)}, u32[]{:S(2)}) collective-permute-start(f32[4,128,128]{2,1,0:T(8,128)S(1)} %bitcast.120), channel_id=1, source_target_pairs={{0,4},{4,8},{8,12},{12,16},{16,20},{20,24},{24,28},{28,0},{1,5},{5... | collective-permute-start | bytes 786440 | tf_op jit(solution)/shard_map/ppermute | solution.py:13
  183.5 14.2 %collective-permute-start.8 = (f32[4,128,128]{2,1,0:T(8,128)S(1)}, f32[4,128,128]{2,1,0:T(8,128)S(1)}, u32[]{:S(2)}, u32[]{:S(2)}) collective-permute-start(f32[4,128,128]{2,1,0:T(8,128)S(1)} %bitcast.121), channel_id=1, source_target_pairs={{0,28},{4,0},{8,4},{12,8},{16,12},{20,16},{24,20},{28,24},{1,29},{... | collective-permute-start | bytes 786440 | tf_op jit(solution)/shard_map/ppermute | solution.py:13
  188.2 12.9 %collective-permute-start.9 = (f32[4,128,128]{2,1,0:T(8,128)S(1)}, f32[4,128,128]{2,1,0:T(8,128)S(1)}, u32[]{:S(2)}, u32[]{:S(2)}) collective-permute-start(f32[4,128,128]{2,1,0:T(8,128)S(1)} %bitcast.122), channel_id=1, source_target_pairs={{0,24},{4,28},{8,0},{12,4},{16,8},{20,12},{24,16},{28,20},{1,25},{... | collective-permute-start | bytes 786440 | tf_op jit(solution)/shard_map/ppermute | solution.py:13
  197.2 5.3 %copy-start.13 = (f32[1,9,128,128]{3,2,1,0:T(8,128)S(1)}, f32[1,9,128,128]{3,2,1,0:T(8,128)}, u32[]{:S(2)}) copy-start(f32[1,9,128,128]{3,2,1,0:T(8,128)} %param.25) | copy-start | bytes 1769476
  226.4 13.8 %collective-permute-start.10 = (f32[1,128,1024]{2,1,0:T(8,128)S(1)}, f32[1,128,1024]{2,1,0:T(8,128)S(1)}, u32[]{:S(2)}, u32[]{:S(2)}) collective-permute-start(f32[1,128,1024]{2,1,0:T(8,128)S(1)} %copy.77), channel_id=1, source_target_pairs={{0,28},{4,0},{8,4},{12,8},{16,12},{20,16},{24,20},{28,24},{1,29},{... | collective-permute-start | bytes 1572872 | tf_op jit(solution)/shard_map/ppermute | solution.py:13
  228.0 12.3 %collective-permute-start.11 = (f32[1,128,1024]{2,1,0:T(8,128)S(1)}, f32[1,128,1024]{2,1,0:T(8,128)S(1)}, u32[]{:S(2)}, u32[]{:S(2)}) collective-permute-start(f32[1,128,1024]{2,1,0:T(8,128)S(1)} %copy.79), channel_id=1, source_target_pairs={{0,3},{1,0},{2,1},{3,2},{4,7},{5,4},{6,5},{7,6},{8,11},{9,8},{10,9... | collective-permute-start | bytes 1572872 | tf_op jit(solution)/shard_map/ppermute | solution.py:13
  283.0 3.6 %copy-start.21 = (f32[128]{0:T(128)}, f32[128]{0:T(128)S(1)}, u32[]{:S(2)}) copy-start(f32[128]{0:T(128)S(1)} %psum.23) | copy-start | bytes 1540
  283.0 3.6 %copy-start.1 = (bf16[1,96,128,128]{3,2,1,0:T(8,128)(2,1)S(1)}, bf16[1,96,128,128]{3,2,1,0:T(8,128)(2,1)}, u32[]{:S(2)}) copy-start(bf16[1,96,128,128]{3,2,1,0:T(8,128)(2,1)} %param.20) | copy-start | bytes 9437188
  (10 other events, 17.2 us)
